TPU v7x, 32 devices: a whole 2x2x4 slice. The times are simulated.
32 devices in a mesh: tm: 4 (over y, x), space: 8 (over z, core).
Axes of the slice: x: 2, y: 2, z: 4, core: 2. Of those that a mesh axis runs over, the one named last changes fastest.
Arguments:
- hidden_in: bfloat16 [8, 16, 32, 5120], P('tm', 'space'), may hold values from -6 to 6
- queries: bfloat16 [8, 16, 32, 5120], P('tm', 'space'), may hold values from -250 to 250
- keys: bfloat16 [8, 16, 32, 5120], P('tm', 'space'), may hold values from -250 to 250
- values: bfloat16 [8, 16, 32, 5120], P('tm', 'space'), may hold values from -6 to 6
- query_gain: float32 [5120], replicated, may hold values from 0.5 to 3
- key_gain: float32 [5120], replicated, may hold values from 0.5 to 3
- reach_time: int32 [40], replicated, may hold values from 0 to 1
- reach_rows: int32 [40], replicated, may hold values from 0 to 1
- reach_cols: int32 [40], replicated, may hold values from 0 to 2
- out_weight: bfloat16 [5120, 5120], P('space', 'tm'), may hold values from -0.25 to 0.25
- gate: float32 [5120], replicated, may hold values from -1.5 to 1.5
Outputs:
- output: bfloat16 [8, 16, 32, 5120], P('tm', 'space')
All inputs are finite; a program needn't handle non-finite values.
Results may differ from a plain program's by a relative error of at most 0.013.
The roundings to bfloat16 on the way count: a program that leaves them out, or rounds other values in their place, can miss the bound.
Values may be sent and summed in bfloat16 or wider, within the bound.
A program may use at most 128 MiB of HBM per device.

v0:
```python
import jax
import jax.numpy as jnp
from jax import lax
from jax.sharding import PartitionSpec as P

TW = 8


def passed_along(block, axis, distance):
    devices = range(lax.axis_size(axis))
    route = [(i - distance, i) for i in devices if i - distance in devices]
    return lax.ppermute(block, axis, route)


def normalize(source, gain):
    values_f = source.astype(jnp.float32)
    mean_square = jnp.mean(values_f * values_f, axis=-1, keepdims=True)
    return (values_f * lax.rsqrt(mean_square + 1e-06) * gain).astype(jnp.bfloat16)


def attend(
    query_block,
    key_region,
    value_region,
    first_frame,
    first_row,
    frame_count,
    row_count,
    reach_time,
    reach_rows,
    reach_cols,
):
    frames_here, rows_here, columns, inner = query_block.shape
    head_count = reach_time.shape[0]
    head_width = inner // head_count
    query_flat = query_block.reshape(-1, head_count, head_width)
    key_flat = key_region.reshape(-1, head_count, head_width)
    value_flat = value_region.reshape(-1, head_count, head_width)
    frame_q = first_frame + jnp.arange(frames_here, dtype=jnp.int32)
    frame_k = first_frame - 1 + jnp.arange(frames_here + 2, dtype=jnp.int32)
    row_q = first_row + jnp.arange(rows_here, dtype=jnp.int32)
    row_k = first_row - 1 + jnp.arange(rows_here + 2, dtype=jnp.int32)
    tiles = jnp.arange(columns, dtype=jnp.int32) // TW
    query_shape = (frames_here, rows_here, columns)
    key_shape = (frames_here + 2, rows_here + 2, columns)
    query_frame = jnp.broadcast_to(frame_q[:, None, None], query_shape).reshape(-1)
    query_row = jnp.broadcast_to(row_q[None, :, None], query_shape).reshape(-1)
    query_tile = jnp.broadcast_to(tiles[None, None, :], query_shape).reshape(-1)
    key_frame = jnp.broadcast_to(frame_k[:, None, None], key_shape).reshape(-1)
    key_row = jnp.broadcast_to(row_k[None, :, None], key_shape).reshape(-1)
    key_tile = jnp.broadcast_to(tiles[None, None, :], key_shape).reshape(-1)
    frame_gap = jnp.abs(query_frame[:, None] - key_frame[None, :])
    row_gap = jnp.abs(query_row[:, None] - key_row[None, :])
    tile_gap = jnp.abs(query_tile[:, None] - key_tile[None, :])
    inside = (key_frame >= 0) & (key_frame < frame_count) & (key_row >= 0) & (key_row < row_count)
    allowed = (frame_gap[None] <= reach_time[:, None, None]) & (
        row_gap[None] <= reach_rows[:, None, None]
    )
    allowed = allowed & (tile_gap[None] <= reach_cols[:, None, None]) & inside[None, None, :]
    scores = jnp.einsum(
        "qhd,khd->hqk", query_flat, key_flat, preferred_element_type=jnp.float32
    ) * head_width ** (-0.5)
    masked = jnp.where(allowed, scores, -jnp.inf)
    row_peak = jnp.max(masked, axis=2, keepdims=True)
    weights = jnp.exp(masked - row_peak)
    totals = jnp.sum(weights, axis=2, keepdims=True)
    rounded = weights.astype(jnp.bfloat16)
    mixed = jnp.einsum("hqk,khd->qhd", rounded, value_flat, preferred_element_type=jnp.float32)
    mixed = mixed / jnp.transpose(totals, (1, 0, 2))
    return mixed.reshape(mixed.shape[0], inner).astype(jnp.bfloat16)


def shards(
    hidden_in,
    queries,
    keys,
    values,
    query_gain,
    key_gain,
    reach_time,
    reach_rows,
    reach_cols,
    out_weight,
    gate,
):
    frames_here, rows_here, columns, inner = queries.shape
    width = hidden_in.shape[3]
    query_norm = normalize(queries, query_gain)
    key_norm = normalize(keys, key_gain)
    stacked = jnp.stack([key_norm, values])
    below_frame = passed_along(stacked[:, -1:], "tm", 1)
    above_frame = passed_along(stacked[:, :1], "tm", -1)
    framed = jnp.concatenate([below_frame, stacked, above_frame], axis=1)
    below_rows = passed_along(framed[:, :, -1:], "space", 1)
    above_rows = passed_along(framed[:, :, :1], "space", -1)
    region = jnp.concatenate([below_rows, framed, above_rows], axis=2)
    first_frame = lax.axis_index("tm") * frames_here
    first_row = lax.axis_index("space") * rows_here
    frame_count = frames_here * lax.axis_size("tm")
    row_count = rows_here * lax.axis_size("space")
    attention = attend(
        query_norm,
        region[0],
        region[1],
        first_frame,
        first_row,
        frame_count,
        row_count,
        reach_time,
        reach_rows,
        reach_cols,
    )
    token_count = attention.shape[0]
    gathered_rows = lax.all_gather(out_weight, "space", axis=0, tiled=True)
    group_terms = jnp.dot(
        lax.all_gather(attention, "tm", axis=0, tiled=True),
        gathered_rows,
        preferred_element_type=jnp.float32,
    )
    branch = lax.all_to_all(group_terms, "tm", split_axis=0, concat_axis=1, tiled=True)
    residual = hidden_in.reshape(token_count, width).astype(jnp.float32)
    output = (residual + gate * branch).astype(jnp.bfloat16)
    return output.reshape(frames_here, rows_here, columns, width)


def solution(mesh):
    in_specs = (
        P("tm", "space", None, None),
        P("tm", "space", None, None),
        P("tm", "space", None, None),
        P("tm", "space", None, None),
        P(),
        P(),
        P(),
        P(),
        P(),
        P("space", "tm"),
        P(),
    )
    out_specs = P("tm", "space", None, None)
    return jax.shard_map(shards, mesh=mesh, in_specs=in_specs, out_specs=out_specs, check_vma=False)
```

profile of v0, /device:TPU:0, one launch (start us, length us, event | category | flops | bytes accessed | tf_op | source)
XLA Modules:
  0.0 403.5 jit_solution(15969228863281141837)
XLA Ops:
  6.5 1.8 fusion.10
  8.3 1.7 fusion.22
  10.0 1.7 fusion.21
  11.8 5.9 %collective-permute-start = (bf16[2,1,2,32,5120]{4,3,2,1,0:T(8,128)(2,1)}, bf16[2,1,2,32,5120]{4,3,2,1,0:T(8,128)(2,1)}, u32[]{:S(2)}, u32[]{:S(2)}) collective-permute-start(bf16[2,1,2,32,5120]{4,3,2,1,0:T(8,128)(2,1)} %get-tuple-element.9), channel_id=1, source_target_pairs={{0,8},{8,16},{16,24},{1,9},{9,17},{17,25},{2,10},{10,18},{18,26},{... | collective-permute-start | bytes 3932168 | tf_op jit(solution)/shard_map/ppermute | solution.py:12
  19.4 25.6 %collective-permute-done = bf16[2,1,2,32,5120]{4,3,2,1,0:T(8,128)(2,1)} collective-permute-done((bf16[2,1,2,32,5120]{4,3,2,1,0:T(8,128)(2,1)}, bf16[2,1,2,32,5120]{4,3,2,1,0:T(8,128)(2,1)}, u32[]{:S(2)}, u32[]{:S(2)}) %collective-permute-start) | collective-permute-done | bytes 1310752 | tf_op jit(solution)/shard_map/ppermute | solution.py:12
  45.0 30.0 %collective-permute-done.1 = bf16[2,1,2,32,5120]{4,3,2,1,0:T(8,128)(2,1)} collective-permute-done((bf16[2,1,2,32,5120]{4,3,2,1,0:T(8,128)(2,1)}, bf16[2,1,2,32,5120]{4,3,2,1,0:T(8,128)(2,1)}, u32[]{:S(2)}, u32[]{:S(2)}) %collective-permute-start.1) | collective-permute-done | bytes 1310752 | tf_op jit(solution)/shard_map/ppermute | solution.py:12
  75.0 2.8 pad_maximum_fusion.1
  77.8 2.8 fusion.25
  80.6 2.7 collective-permute-start.2
  85.2 1.7 fusion.13
  86.9 1.7 fusion.15
  90.9 8.9 %pad_maximum_fusion = bf16[2,4,4,32,5120]{4,3,2,1,0:T(8,128)(2,1)} fusion(bf16[2,4,1,32,5120]{4,3,2,1,0:T(8,128)(2,1)} %collective-permute-done.3, bf16[2,1,2,32,5120]{4,3,2,1,0:T(8,128)(2,1)} %collective-permute-done.1, bf16[1,2,2,32,5120]{4,3,2,1,0:T(8,128)(2,1)S(1)} %bitcast.35, bf16[1,2,2,32,5120]{4,3,2,1,0:T(8,128)(2,1)S(1)} %fusion.22, ...), kind=kLoop, calls=%fused_computation | loop fusion | flops 26214400 | bytes 20971520 | tf_op jit(solution)/shard_map/concatenate | solution.py:96
  99.8 9.1 %fusion.24 = (bf16[1,4,4,32,5120]{4,3,2,1,0:T(8,128)(2,1)}, bf16[1,4,4,32,5120]{4,3,2,1,0:T(8,128)(2,1)}) fusion(bf16[2,4,4,32,5120]{4,3,2,1,0:T(8,128)(2,1)} %pad_maximum_fusion), kind=kLoop, calls=%fused_computation.44 | loop fusion | bytes 20971520 | tf_op jit(solution)/shard_map/slice | solution.py:104
  108.9 4.1 %copy.21 = bf16[64,8,40,128]{3,2,1,0:T(8,128)(2,1)S(1)} copy(bf16[64,8,40,128]{3,1,2,0:T(8,128)(2,1)} %bitcast.32) | data formatting | bytes 10485760
  114.5 4.7 %fusion.26 = (f32[40,128]{1,0:T(8,128)S(1)}, f32[40,128,512]{2,1,0:T(8,128)S(1)}) fusion(bf16[512,40,128]{2,1,0:T(8,128)(2,1)S(1)} %bitcast.38, bf16[128,40,128]{2,1,0:T(8,128)(2,1)S(1)} %bitcast.41, pred[512]{0:T(512)(128)(4,1)S(1)} %compare_and_fusion, s32[40]{0:T(128)S(1)} %copy-done.6, s32[128,512]{1,0:T(8,128)S(1)} %get-tuple-element.13, ...), kind=kOutput, calls=%fused_computation.46 | convolution fusion | flops 694676480 | bytes 17847264 | tf_op jit(solution)/shard_map/qhd,khd->hqk/dot_general | solution.py:60
  119.2 2.4 fusion
  123.2 7.1 %fusion.16 = bf16[128,40,128]{0,2,1:T(8,128)(2,1)} fusion(f32[40,128,512]{2,1,0:T(8,128)} %copy-done.1, f32[40,128]{1,0:T(8,128)S(1)} %get-tuple-element.11, bf16[512,40,128]{2,1,0:T(8,128)(2,1)S(1)} %bitcast.37, f32[128,40]{0,1:T(8,128)S(1)} %bitcast.43), kind=kOutput, calls=%fused_computation.24 | convolution fusion | flops 677642240 | bytes 17080320 | tf_op jit(solution)/shard_map/hqk,khd->qhd/dot_general | solution.py:68
  131.1 86.1 %all-gather.3.cloned.1.call-done = bf16[512,5120]{0,1:T(8,128)(2,1)} async-done(((bf16[128,5120]{0,1:T(8,128)(2,1)}), bf16[512,5120]{0,1:T(8,128)(2,1)}) %all-gather.3.cloned.1.call-update) | async-done | bytes 5242896 | tf_op jit(solution)/shard_map/all_gather | solution.py:116
  217.2 122.7 %all-gather.5.cloned.1.call-done = bf16[5120,1280]{1,0:T(8,128)(2,1)} async-done(((bf16[640,1280]{1,0:T(8,128)(2,1)}), bf16[5120,1280]{1,0:T(8,128)(2,1)}) %all-gather.5.cloned.1.call-update) | async-done | bytes 13107216 | tf_op jit(solution)/shard_map/all_gather | solution.py:114
  339.9 11.5 %fusion.27 = f32[512,1280]{1,0:T(8,128)S(1)} fusion(bf16[512,5120]{0,1:T(8,128)(2,1)} %all-gather.3.cloned.1.call-done, bf16[5120,1280]{1,0:T(8,128)(2,1)} %all-gather.5.cloned.1.call-done), kind=kOutput, calls=%fused_computation.47 | convolution fusion | flops 6710886400 | bytes 20971520 | tf_op jit(solution)/shard_map/dot_general | solution.py:115
  351.4 34.9 %all_to_all.19 = f32[4,128,1280]{2,1,0:T(8,128)S(1)} all-to-all(f32[4,128,1280]{2,1,0:T(8,128)S(1)} %bitcast.40), channel_id=1, replica_groups=mesh['tm'=4,'space'=8] {'tm'}, dimensions={0} | all-to-all | bytes 5242880 | tf_op jit(solution)/shard_map/all_to_all | solution.py:120
  386.2 3.2 copy.18
  389.4 4.1 %all_to_all.17 = f32[2,2,32,5120]{3,2,1,0:T(8,128)} reshape(f32[128,4,1280]{2,1,0:T(4,128)} %copy.18) | data formatting | bytes 5242880 | tf_op jit(solution)/shard_map/all_to_all | solution.py:120
  393.5 3.1 add_convert_fusion
  (55 shorter events, 9.5 us)
Async XLA Ops:
  6.5 3.5 copy-start
  6.5 210.6 %all-gather.3.cloned.1.call-start = ((), (), s32[]{:S(2)}) async-start(), calls=%async_computation.1 | async-start | bytes 6553600 | tf_op jit(solution)/shard_map/all_gather | solution.py:116
  11.8 33.2 %collective-permute-start = (bf16[2,1,2,32,5120]{4,3,2,1,0:T(8,128)(2,1)}, bf16[2,1,2,32,5120]{4,3,2,1,0:T(8,128)(2,1)}, u32[]{:S(2)}, u32[]{:S(2)}) collective-permute-start(bf16[2,1,2,32,5120]{4,3,2,1,0:T(8,128)(2,1)} %get-tuple-element.9), channel_id=1, source_target_pairs={{0,8},{8,16},{16,24},{1,9},{9,17},{17,25},{2,10},{10,18},{18,26},{... | collective-permute-start | bytes 3932168 | tf_op jit(solution)/shard_map/ppermute | solution.py:12
  17.7 57.3 %collective-permute-start.1 = (bf16[2,1,2,32,5120]{4,3,2,1,0:T(8,128)(2,1)}, bf16[2,1,2,32,5120]{4,3,2,1,0:T(8,128)(2,1)}, u32[]{:S(2)}, u32[]{:S(2)}) collective-permute-start(bf16[2,1,2,32,5120]{4,3,2,1,0:T(8,128)(2,1)} %get-tuple-element.10), channel_id=1, source_target_pairs={{8,0},{16,8},{24,16},{9,1},{17,9},{25,17},{10,2},{18,10},{26,18},{... | collective-permute-start | bytes 3932168 | tf_op jit(solution)/shard_map/ppermute | solution.py:12
  77.8 9.0 %copy-start.4 = (f32[5120]{0:T(1024)S(1)}, f32[5120]{0:T(1024)}, u32[]{:S(2)}) copy-start(f32[5120]{0:T(1024)} %param.15) | copy-start | bytes 61444
  80.6 9.5 %collective-permute-start.2 = (bf16[2,4,1,32,5120]{4,3,2,1,0:T(8,128)(2,1)}, bf16[2,4,1,32,5120]{4,3,2,1,0:T(8,128)(2,1)}, u32[]{:S(2)}, u32[]{:S(2)}) collective-permute-start(bf16[2,4,1,32,5120]{4,3,2,1,0:T(8,128)(2,1)} %get-tuple-element.7), channel_id=1, source_target_pairs={{0,1},{1,2},{2,3},{3,4},{4,5},{5,6},{6,7},{8,9},{9,10},{10,11},{11... | collective-permute-start | bytes 7864328 | tf_op jit(solution)/shard_map/ppermute | solution.py:12
  83.4 7.5 %collective-permute-start.3 = (bf16[2,4,1,32,5120]{4,3,2,1,0:T(8,128)(2,1)}, bf16[2,4,1,32,5120]{4,3,2,1,0:T(8,128)(2,1)}, u32[]{:S(2)}, u32[]{:S(2)}) collective-permute-start(bf16[2,4,1,32,5120]{4,3,2,1,0:T(8,128)(2,1)} %get-tuple-element.8), channel_id=1, source_target_pairs={{1,0},{2,1},{3,2},{4,3},{5,4},{6,5},{7,6},{9,8},{10,9},{11,10},{12... | collective-permute-start | bytes 7864328 | tf_op jit(solution)/shard_map/ppermute | solution.py:12
  108.9 4.1 %slice-start = ((s8[5242880]{0:T(1024)(128)(4,1)}), s8[4194304]{0:T(1024)(128)(4,1)S(1)}, s32[]{:S(2)}) async-start(s8[5242880]{0:T(1024)(128)(4,1)} %bitcast.29), calls=%async_computation.3 | async-start | bytes 8388608
  108.9 4.1 %slice-start.1 = ((s8[5242880]{0:T(1024)(128)(4,1)}), s8[1048576]{0:T(1024)(128)(4,1)S(1)}, s32[]{:S(2)}) async-start(s8[5242880]{0:T(1024)(128)(4,1)} %bitcast.29), calls=%async_computation.4 | async-start | bytes 2097152
  113.0 1.5 copy-start.2
  113.0 1.5 copy-start.6
  113.0 1.5 copy-start.7
  113.0 1.5 copy-start.8
  119.2 4.0 copy-start.1
  130.3 209.6 %all-gather.5.cloned.1.call-start = ((), (), s32[]{:S(2)}) async-start(), calls=%async_computation.2 | async-start | bytes 14745600 | tf_op jit(solution)/shard_map/all_gather | solution.py:114
  389.4 4.1 %copy-start.3 = (bf16[2,2,32,5120]{3,2,1,0:T(8,128)(2,1)S(1)}, bf16[2,2,32,5120]{3,2,1,0:T(8,128)(2,1)}, u32[]{:S(2)}) copy-start(bf16[2,2,32,5120]{3,2,1,0:T(8,128)(2,1)} %param.11) | copy-start | bytes 3932164
  389.4 4.1 %copy-start.5 = (f32[5120]{0:T(1024)S(1)}, f32[5120]{0:T(1024)}, u32[]{:S(2)}) copy-start(f32[5120]{0:T(1024)} %param.21) | copy-start | bytes 61444
Sparse Core Ops, SparseCore 0:
  130.4 86.7 all-gather.2
  218.8 120.9 all-gather.4
where the time goes:
time: 404 us
  waiting for transfers between devices  266 us (66%)
  blocking collectives  34.9 us (9%)
  local copies, waits for them, and re-layouts  28.3 us (7%)
  other arithmetic  26.2 us (6%)
  matrix products  23.3 us (6%)
  between operations  13.7 us (3%)
  starting transfers between devices  11.3 us (3%)
    all_gather x1, waiting for transfers between devices, shards(): gathered_rows = lax.all_gather(out_weight, 'space', axis=0, tiled=True)  123 us
    all_gather x1, waiting for transfers between devices, shards(): lax.all_gather(attention, 'tm', axis=0, tiled=True)  86.1 us
    ppermute x4, waiting for transfers between devices, passed_along(): return lax.ppermute(block, axis, route)  56.4 us
    all_to_all x1, blocking collectives, shards(): lax.all_to_all(group_terms, 'tm', split_axis=0, concat_axis=1, tiled=True)  34.9 us
    dot_general x1, matrix products, shards(): jnp.dot(lax.all_gather(attention, 'tm', axis=0, tiled=True), gathered_row...  11.5 us
    ppermute x4, starting transfers between devices, passed_along(): return lax.ppermute(block, axis, route)  11.3 us
    slice x1, local copies, waits for them, and re-layouts, shards(): region[1]  9.06 us
    concatenate x1, other arithmetic, shards(): region = jnp.concatenate([below_rows, framed, above_rows], axis=2)  8.94 us
  transfers between devices with their start and end apart: 6, of which 5 were waited for; matrix products, arithmetic and copies ran while one was open for 1% of the time, Pallas kernels for 0%

commit v1 on v0

--- a/solution.py
+++ b/solution.py
@@ -90,9 +90,14 @@
     stacked = jnp.stack([key_norm, values])
     below_frame = passed_along(stacked[:, -1:], "tm", 1)
     above_frame = passed_along(stacked[:, :1], "tm", -1)
+    below_own = passed_along(stacked[:, :, -1:], "space", 1)
+    above_own = passed_along(stacked[:, :, :1], "space", -1)
+    margins = jnp.concatenate([below_frame, above_frame], axis=1)
+    below_margin = passed_along(margins[:, :, -1:], "space", 1)
+    above_margin = passed_along(margins[:, :, :1], "space", -1)
     framed = jnp.concatenate([below_frame, stacked, above_frame], axis=1)
-    below_rows = passed_along(framed[:, :, -1:], "space", 1)
-    above_rows = passed_along(framed[:, :, :1], "space", -1)
+    below_rows = jnp.concatenate([below_margin[:, :1], below_own, below_margin[:, 1:]], axis=1)
+    above_rows = jnp.concatenate([above_margin[:, :1], above_own, above_margin[:, 1:]], axis=1)
     region = jnp.concatenate([below_rows, framed, above_rows], axis=2)
     first_frame = lax.axis_index("tm") * frames_here
     first_row = lax.axis_index("space") * rows_here
@@ -112,14 +117,15 @@
     )
     token_count = attention.shape[0]
     gathered_rows = lax.all_gather(out_weight, "space", axis=0, tiled=True)
+    attention, gathered_rows = lax.optimization_barrier((attention, gathered_rows))
     group_terms = jnp.dot(
         lax.all_gather(attention, "tm", axis=0, tiled=True),
         gathered_rows,
         preferred_element_type=jnp.float32,
-    )
+    ).astype(jnp.bfloat16)
     branch = lax.all_to_all(group_terms, "tm", split_axis=0, concat_axis=1, tiled=True)
     residual = hidden_in.reshape(token_count, width).astype(jnp.float32)
-    output = (residual + gate * branch).astype(jnp.bfloat16)
+    output = (residual + gate * branch.astype(jnp.float32)).astype(jnp.bfloat16)
     return output.reshape(frames_here, rows_here, columns, width)
 
 

time: 404 us -> 305 us (0.75)
  waiting for transfers between devices: 266 us -> 182 us
  blocking collectives: 34.9 us -> 19.5 us
    all_gather x1, waiting for transfers between devices: 123 us -> 31.1 us  [shards(): gathered_rows = lax.all_gather(out_weight, 'space', axis=0, tiled=True)]
    all_to_all x1, blocking collectives: 34.9 us -> 19.5 us  [shards(): lax.all_to_all(group_terms, 'tm', split_axis=0, concat_axis=1, tiled=True)]
    all_gather x1, waiting for transfers between devices: 86.1 us -> 98.4 us  [shards(): lax.all_gather(attention, 'tm', axis=0, tiled=True)]
    all_to_all x2 -> x0, local copies, waits for them, and re-layouts: 7.29 us -> none  [shards(): lax.all_to_all(group_terms, 'tm', split_axis=0, concat_axis=1, tiled=True)]
    convert_element_type x0 -> x2, local copies, waits for them, and re-layouts: none -> 6.24 us  [shards(): output = (residual + gate * branch.astype(jnp.float32)).astype(jnp.bfloat16)]
    ppermute x4 -> x6, waiting for transfers between devices: 56.4 us -> 51.5 us  [passed_along(): return lax.ppermute(block, axis, route)]
    ppermute x4 -> x6, starting transfers between devices: 11.3 us -> 14 us  [passed_along(): return lax.ppermute(block, axis, route)]
    unnamed x25 -> x32, local copies, waits for them, and re-layouts: 8.41 us -> 9.79 us
  transfers between devices with their start and end apart: 6 -> 8, of which waited for: 5 -> 5; matrix products, arithmetic and copies ran while one was open for 1% -> 17% of each run, Pallas kernels for 0% -> 0%
where the time goes in v1:
time: 305 us; the launch traced here: 304 us
  waiting for transfers between devices  182 us (60%)
  local copies, waits for them, and re-layouts  28 us (9%)
  matrix products  25 us (8%)
  other arithmetic  22.4 us (7%)
  blocking collectives  19.5 us (6%)
  starting transfers between devices  14 us (5%)
  between operations  13.8 us (5%)
    all_gather x1, waiting for transfers between devices, shards(): lax.all_gather(attention, 'tm', axis=0, tiled=True)  98.4 us
    ppermute x6, waiting for transfers between devices, passed_along(): return lax.ppermute(block, axis, route)  51.5 us
    all_gather x1, waiting for transfers between devices, shards(): gathered_rows = lax.all_gather(out_weight, 'space', axis=0, tiled=True)  31.1 us
    all_to_all x1, blocking collectives, shards(): lax.all_to_all(group_terms, 'tm', split_axis=0, concat_axis=1, tiled=True)  19.5 us
    ppermute x6, starting transfers between devices, passed_along(): return lax.ppermute(block, axis, route)  14 us
    dot_general x1, matrix products, shards(): jnp.dot(lax.all_gather(attention, 'tm', axis=0, tiled=True), gathered_row...  12.7 us
    unnamed x32, local copies, waits for them, and re-layouts  9.79 us
    slice x1, local copies, waits for them, and re-layouts, shards(): region[1]  9.33 us
  transfers between devices with their start and end apart: 8, of which 5 were waited for; matrix products, arithmetic and copies ran while one was open for 17% of the time, Pallas kernels for 0%

profile of v1, /device:TPU:0, one launch (start us, length us, event | category | flops | bytes accessed | tf_op | source)
XLA Modules:
  0.0 304.5 jit_solution(2186317518982047094)
XLA Ops:
  7.3 1.7 fusion.10
  9.0 1.7 fusion.21
  10.7 1.7 fusion.24
  12.4 6.0 %collective-permute-start = (bf16[2,1,2,32,5120]{4,3,2,1,0:T(8,128)(2,1)}, bf16[2,1,2,32,5120]{4,3,2,1,0:T(8,128)(2,1)}, u32[]{:S(2)}, u32[]{:S(2)}) collective-permute-start(bf16[2,1,2,32,5120]{4,3,2,1,0:T(8,128)(2,1)} %get-tuple-element.16), channel_id=1, source_target_pairs={{0,8},{8,16},{16,24},{1,9},{9,17},{17,25},{2,10},{10,18},{18,26},{... | collective-permute-start | bytes 3932168 | tf_op jit(solution)/shard_map/ppermute | solution.py:12
  19.7 1.7 fusion.22
  21.4 2.5 collective-permute-start.3
  26.1 1.7 fusion.13
  27.8 17.9 %collective-permute-done = bf16[2,1,2,32,5120]{4,3,2,1,0:T(8,128)(2,1)} collective-permute-done((bf16[2,1,2,32,5120]{4,3,2,1,0:T(8,128)(2,1)}, bf16[2,1,2,32,5120]{4,3,2,1,0:T(8,128)(2,1)}, u32[]{:S(2)}, u32[]{:S(2)}) %collective-permute-start) | collective-permute-done | bytes 1310752 | tf_op jit(solution)/shard_map/ppermute | solution.py:12
  47.0 28.6 %collective-permute-done.1 = bf16[2,1,2,32,5120]{4,3,2,1,0:T(8,128)(2,1)} collective-permute-done((bf16[2,1,2,32,5120]{4,3,2,1,0:T(8,128)(2,1)}, bf16[2,1,2,32,5120]{4,3,2,1,0:T(8,128)(2,1)}, u32[]{:S(2)}, u32[]{:S(2)}) %collective-permute-start.1) | collective-permute-done | bytes 1310752 | tf_op jit(solution)/shard_map/ppermute | solution.py:12
  83.3 5.0 %collective-permute-done.4 = bf16[2,2,1,32,5120]{4,3,2,1,0:T(8,128)(2,1)S(1)} collective-permute-done((bf16[2,2,1,32,5120]{4,3,2,1,0:T(8,128)(2,1)S(1)}, bf16[2,2,1,32,5120]{4,3,2,1,0:T(8,128)(2,1)S(1)}, u32[]{:S(2)}, u32[]{:S(2)}) %collective-permute-start.4) | collective-permute-done | bytes 1310752 | tf_op jit(solution)/shard_map/ppermute | solution.py:12
  88.3 7.1 %maximum_maximum_fusion = bf16[2,4,4,32,5120]{4,3,2,1,0:T(8,128)(2,1)} fusion(bf16[2,1,1,32,5120]{4,3,2,1,0:T(8,128)(2,1)S(1)} %get-tuple-element.20, bf16[2,2,1,32,5120]{4,3,2,1,0:T(8,128)(2,1)} %collective-permute-done.5, bf16[2,1,1,32,5120]{4,3,2,1,0:T(8,128)(2,1)S(1)} %get-tuple-element.19, bf16[2,1,2,32,5120]{4,3,2,1,0:T(8,128)(2,1)} %collective-permute-done.1, ...), kind=kLoop, calls=%fused_computation | loop fusion | flops 47185920 | bytes 20971520 | tf_op jit(solution)/shard_map/concatenate | solution.py:101
  95.4 9.3 %fusion.26 = (bf16[1,4,4,32,5120]{4,3,2,1,0:T(8,128)(2,1)}, bf16[1,4,4,32,5120]{4,3,2,1,0:T(8,128)(2,1)}) fusion(bf16[2,4,4,32,5120]{4,3,2,1,0:T(8,128)(2,1)} %maximum_maximum_fusion), kind=kLoop, calls=%fused_computation.53 | loop fusion | bytes 20971520 | tf_op jit(solution)/shard_map/slice | solution.py:109
  104.8 4.1 %copy.21 = bf16[64,8,40,128]{3,2,1,0:T(8,128)(2,1)S(1)} copy(bf16[64,8,40,128]{3,1,2,0:T(8,128)(2,1)} %bitcast.33) | data formatting | bytes 10485760
  110.5 5.1 %fusion.30 = (f32[40,128]{1,0:T(8,128)S(1)}, f32[40,128,512]{2,1,0:T(8,128)S(1)}) fusion(bf16[512,40,128]{2,1,0:T(8,128)(2,1)S(1)} %bitcast.38, bf16[128,40,128]{2,1,0:T(8,128)(2,1)S(1)} %bitcast.40, pred[512]{0:T(512)(128)(4,1)S(1)} %compare_and_fusion, s32[40]{0:T(128)S(1)} %copy-done.9, s32[128,512]{1,0:T(8,128)S(1)} %copy-done.4, s32[40]{0:T(128)S(1)} %copy-done.10, ...), kind=kOutput, calls=%fused_computation.57 | convolution fusion | flops 694676480 | bytes 17847264 | tf_op jit(solution)/shard_map/qhd,khd->hqk/dot_general | solution.py:60
  115.5 2.4 fusion
  117.9 1.5 copy-done.1
  119.5 7.2 %fusion.16 = bf16[128,40,128]{0,2,1:T(8,128)(2,1)} fusion(f32[40,128,512]{2,1,0:T(8,128)} %copy-done.1, f32[40,128]{1,0:T(8,128)S(1)} %get-tuple-element.21, bf16[512,40,128]{2,1,0:T(8,128)(2,1)S(1)} %bitcast.37, f32[128,40]{0,1:T(8,128)S(1)} %bitcast.43), kind=kOutput, calls=%fused_computation.28 | convolution fusion | flops 677642240 | bytes 17080320 | tf_op jit(solution)/shard_map/hqk,khd->qhd/dot_general | solution.py:68
  126.7 31.1 %all-gather.3.cloned.1.call-done = bf16[5120,1280]{1,0:T(8,128)(2,1)} async-done(((bf16[640,1280]{1,0:T(8,128)(2,1)}), bf16[5120,1280]{1,0:T(8,128)(2,1)}) %all-gather.3.cloned.1.call-update) | async-done | bytes 13107216 | tf_op jit(solution)/shard_map/all_gather | solution.py:119
  157.8 98.4 %all-gather.5.cloned.1.call-done = bf16[512,5120]{0,1:T(8,128)(2,1)} async-done(((bf16[128,5120]{0,1:T(8,128)(2,1)}), bf16[512,5120]{0,1:T(8,128)(2,1)}) %all-gather.5.cloned.1.call-update) | async-done | bytes 5242896 | tf_op jit(solution)/shard_map/all_gather | solution.py:122
  256.2 12.7 %convolution_convert_fusion = bf16[512,1280]{1,0:T(8,128)(2,1)S(1)} fusion(bf16[512,5120]{0,1:T(8,128)(2,1)} %all-gather.5.cloned.1.call-done, bf16[5120,1280]{1,0:T(8,128)(2,1)} %all-gather.3.cloned.1.call-done), kind=kOutput, calls=%fused_computation.20 | convolution fusion | flops 6711541760 | bytes 19660800 | tf_op jit(solution)/shard_map/dot_general | solution.py:121
  268.9 19.5 %all_to_all.13 = bf16[4,128,1280]{2,1,0:T(8,128)(2,1)S(1)} all-to-all(bf16[4,128,1280]{2,1,0:T(8,128)(2,1)S(1)} %bitcast.42), channel_id=1, replica_groups=mesh['tm'=4,'space'=8] {'tm'}, dimensions={0} | all-to-all | bytes 2621440 | tf_op jit(solution)/shard_map/all_to_all | solution.py:126
  288.7 3.2 %copy.18 = f32[128,4,1280]{2,1,0:T(4,128)} copy(f32[128,4,1280]{2,0,1:T(8,128)S(1)} %convert_bitcast_fusion) | data formatting | bytes 5242880 | tf_op jit(solution)/shard_map/convert_element_type | solution.py:128
  291.9 3.0 reshape.196
  294.9 2.7 add_convert_fusion
  (70 shorter events, 14.9 us)
Async XLA Ops:
  6.5 2.5 copy-start.6
  6.5 4.2 %copy-start = (bf16[2,2,32,5120]{3,2,1,0:T(8,128)(2,1)S(1)}, bf16[2,2,32,5120]{3,2,1,0:T(8,128)(2,1)}, u32[]{:S(2)}) copy-start(bf16[2,2,32,5120]{3,2,1,0:T(8,128)(2,1)} %param.14) | copy-start | bytes 3932164
  6.5 151.2 %all-gather.3.cloned.1.call-start = ((), (), s32[]{:S(2)}) async-start(), calls=%async_computation.1 | async-start | bytes 14745600 | tf_op jit(solution)/shard_map/all_gather | solution.py:119
  7.3 248.9 %all-gather.5.cloned.1.call-start = ((), (), s32[]{:S(2)}) async-start(), calls=%async_computation.2 | async-start | bytes 6553600 | tf_op jit(solution)/shard_map/all_gather | solution.py:122
  12.4 33.2 %collective-permute-start = (bf16[2,1,2,32,5120]{4,3,2,1,0:T(8,128)(2,1)}, bf16[2,1,2,32,5120]{4,3,2,1,0:T(8,128)(2,1)}, u32[]{:S(2)}, u32[]{:S(2)}) collective-permute-start(bf16[2,1,2,32,5120]{4,3,2,1,0:T(8,128)(2,1)} %get-tuple-element.16), channel_id=1, source_target_pairs={{0,8},{8,16},{16,24},{1,9},{9,17},{17,25},{2,10},{10,18},{18,26},{... | collective-permute-start | bytes 3932168 | tf_op jit(solution)/shard_map/ppermute | solution.py:12
  18.4 57.3 %collective-permute-start.1 = (bf16[2,1,2,32,5120]{4,3,2,1,0:T(8,128)(2,1)}, bf16[2,1,2,32,5120]{4,3,2,1,0:T(8,128)(2,1)}, u32[]{:S(2)}, u32[]{:S(2)}) collective-permute-start(bf16[2,1,2,32,5120]{4,3,2,1,0:T(8,128)(2,1)} %get-tuple-element.15), channel_id=1, source_target_pairs={{8,0},{16,8},{24,16},{9,1},{17,9},{25,17},{10,2},{18,10},{26,18},{... | collective-permute-start | bytes 3932168 | tf_op jit(solution)/shard_map/ppermute | solution.py:12
  21.4 66.9 %collective-permute-start.3 = (bf16[2,2,1,32,5120]{4,3,2,1,0:T(8,128)(2,1)}, bf16[2,2,1,32,5120]{4,3,2,1,0:T(8,128)(2,1)}, u32[]{:S(2)}, u32[]{:S(2)}) collective-permute-start(bf16[2,2,1,32,5120]{4,3,2,1,0:T(8,128)(2,1)} %get-tuple-element.11), channel_id=1, source_target_pairs={{0,1},{1,2},{2,3},{3,4},{4,5},{5,6},{6,7},{8,9},{9,10},{10,11},{11... | collective-permute-start | bytes 3932168 | tf_op jit(solution)/shard_map/ppermute | solution.py:12
  23.9 64.4 %collective-permute-start.5 = (bf16[2,2,1,32,5120]{4,3,2,1,0:T(8,128)(2,1)}, bf16[2,2,1,32,5120]{4,3,2,1,0:T(8,128)(2,1)}, u32[]{:S(2)}, u32[]{:S(2)}) collective-permute-start(bf16[2,2,1,32,5120]{4,3,2,1,0:T(8,128)(2,1)} %get-tuple-element.12), channel_id=1, source_target_pairs={{1,0},{2,1},{3,2},{4,3},{5,4},{6,5},{7,6},{9,8},{10,9},{11,10},{12... | collective-permute-start | bytes 3932168 | tf_op jit(solution)/shard_map/ppermute | solution.py:12
  77.2 1.7 copy-start.2
  77.2 1.7 copy-start.7
  77.4 5.8 %collective-permute-start.2 = (bf16[2,2,1,32,5120]{4,3,2,1,0:T(8,128)(2,1)S(1)}, bf16[2,2,1,32,5120]{4,3,2,1,0:T(8,128)(2,1)S(1)}, u32[]{:S(2)}, u32[]{:S(2)}) collective-permute-start(bf16[2,2,1,32,5120]{4,3,2,1,0:T(8,128)(2,1)S(1)} %get-tuple-element.13), channel_id=1, source_target_pairs={{0,1},{1,2},{2,3},{3,4},{4,5},{5,6},{6,7},{8,9},{9,10},{10,11},{11... | collective-permute-start | bytes 3932168 | tf_op jit(solution)/shard_map/ppermute | solution.py:12
  81.7 6.6 %collective-permute-start.4 = (bf16[2,2,1,32,5120]{4,3,2,1,0:T(8,128)(2,1)S(1)}, bf16[2,2,1,32,5120]{4,3,2,1,0:T(8,128)(2,1)S(1)}, u32[]{:S(2)}, u32[]{:S(2)}) collective-permute-start(bf16[2,2,1,32,5120]{4,3,2,1,0:T(8,128)(2,1)S(1)} %get-tuple-element.14), channel_id=1, source_target_pairs={{1,0},{2,1},{3,2},{4,3},{5,4},{6,5},{7,6},{9,8},{10,9},{11,10},{12... | collective-permute-start | bytes 3932168 | tf_op jit(solution)/shard_map/ppermute | solution.py:12
  104.8 4.1 %slice-start = ((s8[5242880]{0:T(1024)(128)(4,1)}), s8[4194304]{0:T(1024)(128)(4,1)S(1)}, s32[]{:S(2)}) async-start(s8[5242880]{0:T(1024)(128)(4,1)} %bitcast.30), calls=%async_computation.3 | async-start | bytes 8388608
  104.8 4.1 %slice-start.1 = ((s8[5242880]{0:T(1024)(128)(4,1)}), s8[1048576]{0:T(1024)(128)(4,1)S(1)}, s32[]{:S(2)}) async-start(s8[5242880]{0:T(1024)(128)(4,1)} %bitcast.30), calls=%async_computation.4 | async-start | bytes 2097152
  108.9 1.5 copy-start.3
  108.9 1.5 copy-start.4
  108.9 1.5 copy-start.5
  108.9 1.5 copy-start.9
  108.9 1.5 copy-start.10
  108.9 1.5 copy-start.11
  115.5 3.9 %copy-start.1 = (f32[40,128,512]{2,1,0:T(8,128)}, f32[40,128,512]{2,1,0:T(8,128)S(1)}, u32[]{:S(2)}) copy-start(f32[40,128,512]{2,1,0:T(8,128)S(1)} %get-tuple-element.22) | copy-start | bytes 31457284
  291.9 3.1 %copy-start.8 = (f32[5120]{0:T(1024)S(1)}, f32[5120]{0:T(1024)}, u32[]{:S(2)}) copy-start(f32[5120]{0:T(1024)} %param.21) | copy-start | bytes 61444
Sparse Core Ops, SparseCore 0:
  9.0 148.7 all-gather.2
  159.6 96.5 all-gather.4

commit v2 on v0

v2 whole, which is shorter than its diff:
```python
import functools
import math

import jax
import jax.numpy as jnp
from jax import lax
from jax.experimental import pallas as pl
from jax.experimental.pallas import tpu as pltpu
from jax.sharding import PartitionSpec as P

TW = 8
REACHES = [(a, b, c) for a in range(2) for b in range(2) for c in range(3)]


def normalize(source, gain):
    values_f = source.astype(jnp.float32)
    mean_square = jnp.mean(values_f * values_f, axis=-1, keepdims=True)
    return (values_f * lax.rsqrt(mean_square + 1e-06) * gain).astype(jnp.bfloat16)


def mask_table(frames_here, rows_here, columns, first_frame, first_row, frame_count, row_count):
    query_shape = (frames_here, rows_here, columns)
    key_shape = (frames_here + 2, rows_here + 2, columns)

    def spread(vector, axis, shape):
        dims = [1, 1, 1]
        dims[axis] = vector.shape[0]
        return jnp.broadcast_to(vector.reshape(dims), shape).reshape(-1)

    tiles = jnp.arange(columns, dtype=jnp.int32) // TW
    query_parts = (
        spread(first_frame + jnp.arange(frames_here, dtype=jnp.int32), 0, query_shape),
        spread(first_row + jnp.arange(rows_here, dtype=jnp.int32), 1, query_shape),
        spread(tiles, 2, query_shape),
    )
    key_parts = (
        spread(first_frame - 1 + jnp.arange(frames_here + 2, dtype=jnp.int32), 0, key_shape),
        spread(first_row - 1 + jnp.arange(rows_here + 2, dtype=jnp.int32), 1, key_shape),
        spread(tiles, 2, key_shape),
    )
    inside = (
        (key_parts[0] >= 0)
        & (key_parts[0] < frame_count)
        & (key_parts[1] >= 0)
        & (key_parts[1] < row_count)
    )
    gaps = [jnp.abs(q[:, None] - k[None, :]) for q, k in zip(query_parts, key_parts)]
    reach = jnp.array(REACHES, jnp.int32)
    allowed = inside[None, None, :]
    for axis in range(3):
        allowed = allowed & (gaps[axis][None] <= reach[:, axis][:, None, None])
    return jnp.where(allowed, 0.0, -1e30).astype(jnp.float32)


def kernel(
    heads,
    group,
    kind_ref,
    query_ref,
    mask_ref,
    hidden_ref,
    gate_ref,
    kv_ref,
    weight_ref,
    out_ref,
    region,
    weights,
    mixed,
    total,
    outgoing,
    incoming,
    local_sem,
    halo_send,
    halo_recv,
    near_send,
    pair_send,
    weight_recv,
    mixed_send,
    mixed_recv,
    back_send,
    back_recv,
):
    t = lax.axis_index("tm")
    s = lax.axis_index("space")
    nt = lax.axis_size("tm")
    ns = lax.axis_size("space")
    chips = ns // 2
    frames, rows, columns, inner = kv_ref.shape[1:]
    tokens = frames * rows * columns
    keys_here = (frames + 2) * (rows + 2) * columns
    width = inner // heads
    depth, cols = weight_ref.shape

    def remote(source, target, send, recv, tm, space):
        return pltpu.make_async_remote_copy(
            src_ref=source,
            dst_ref=target,
            send_sem=send,
            recv_sem=recv,
            device_id=(tm, space),
            device_id_type=pl.DeviceIdType.MESH,
        )

    has_low_t, has_high_t = t > 0, t < nt - 1
    has_low_s, has_high_s = s > 0, s < ns - 1
    own_f, own_r = pl.ds(1, frames), pl.ds(1, rows)

    def halo(i, source, target, tm, space):
        return remote(source, target, halo_send.at[i], halo_recv.at[i], tm, space)

    up_f = halo(0, kv_ref.at[:, frames - 1], region.at[:, 0, own_r], t + 1, s)
    down_f = halo(1, kv_ref.at[:, 0], region.at[:, frames + 1, own_r], t - 1, s)
    up_r = halo(2, kv_ref.at[:, :, rows - 1], region.at[:, own_f, 0], t, s + 1)
    down_r = halo(3, kv_ref.at[:, :, 0], region.at[:, own_f, rows + 1], t, s - 1)
    corners = []
    for i, (frame, has_frame) in enumerate(((0, has_low_t), (frames + 1, has_high_t))):
        corners.append((
            halo(4 + 2 * i, region.at[:, frame, rows], region.at[:, frame, 0], t, s + 1),
            has_frame & has_high_s, has_frame & has_low_s,
        ))
        corners.append((
            halo(5 + 2 * i, region.at[:, frame, 1], region.at[:, frame, rows + 1], t, s - 1),
            has_frame & has_low_s, has_frame & has_high_s,
        ))
    straight = [
        (up_f, has_high_t, has_low_t),
        (down_f, has_low_t, has_high_t),
        (up_r, has_high_s, has_low_s),
        (down_r, has_low_s, has_high_s),
    ]

    def block(ref, b):
        return ref.at[pl.ds(pl.multiple_of(b * depth, depth), depth)]

    partner = s + 1 - 2 * lax.rem(s, 2)

    def near(k, b, way, first):
        space = s + 2 if way == 0 else s - 2
        source = weight_ref if first else block(weights, b)
        return remote(source, block(weights, b), near_send.at[way, k], weight_recv.at[b], t, space)

    def pair(k, b, way, first):
        source = weight_ref if first else block(weights, b)
        return remote(source, block(weights, b), pair_send.at[way, k], weight_recv.at[b], t, partner)

    def arrived(b):
        remote(block(weights, b), block(weights, b), pair_send.at[0, 0], weight_recv.at[b], t, partner).wait_recv()

    for copy, sends, _ in straight:
        pl.when(sends)(copy.start)
    pl.when(s + 2 < ns)(near(0, s, 0, True).start)
    pl.when(s >= 2)(near(0, s, 1, True).start)
    pair(0, s, 0, True).start()
    own_kv = pltpu.make_async_copy(kv_ref, region.at[:, own_f, own_r], local_sem.at[0])
    own_kv.start()
    own_weight = pltpu.make_async_copy(weight_ref, block(weights, s), local_sem.at[1])
    own_weight.start()

    def clear_frame(frame):
        def run():
            for part in range(2):
                for row in range(rows + 2):
                    region[part, frame, row] = jnp.zeros((columns, inner), jnp.bfloat16)
        return run

    def clear_row(row):
        def run():
            for part in range(2):
                for frame in range(frames + 2):
                    region[part, frame, row] = jnp.zeros((columns, inner), jnp.bfloat16)
        return run

    pl.when(jnp.logical_not(has_low_t))(clear_frame(0))
    pl.when(jnp.logical_not(has_high_t))(clear_frame(frames + 1))
    pl.when(jnp.logical_not(has_low_s))(clear_row(0))
    pl.when(jnp.logical_not(has_high_s))(clear_row(rows + 1))

    def relay(k):
        low, high = s - 2 * k, s + 2 * k

        @pl.when(low >= 0)
        def _():
            arrived(low)
            pl.when(s + 2 < ns)(near(k, low, 0, False).start)
            pair(k, low, 0, False).start()

        @pl.when(high < ns)
        def _():
            arrived(high)
            pl.when(s >= 2)(near(k, high, 1, False).start)
            pair(k, high, 1, False).start()

    for copy, _, receives in straight[:2]:
        pl.when(receives)(copy.wait_recv)
    for copy, sends, _ in corners:
        pl.when(sends)(copy.start)
    relay(1)
    for copy, _, receives in straight[2:]:
        pl.when(receives)(copy.wait_recv)
    for copy, _, receives in corners:
        pl.when(receives)(copy.wait_recv)
    own_kv.wait()

    groups = heads // group
    span = group * width

    def gather(g, d):
        at = (t, slice(None), pl.ds(pl.multiple_of(g * span, span), span))
        return remote(
            mixed.at[at], mixed.at[at], mixed_send.at[d - 1, g], mixed_recv.at[t, g],
            lax.rem(t + d, nt), s,
        )

    def one_group(g, carry):
        for i in range(group):
            h = g * group + i
            lanes = pl.ds(pl.multiple_of(h * width, width), width)
            query = query_ref[:, lanes]
            key = region[0, :, :, :, lanes].reshape(keys_here, width)
            value = region[1, :, :, :, lanes].reshape(keys_here, width)
            scores = lax.dot_general(
                query, key, (((1,), (1,)), ((), ())), preferred_element_type=jnp.float32
            ) * width ** (-0.5)
            scores = scores + mask_ref[kind_ref[h]]
            part = jnp.exp(scores - jnp.max(scores, axis=1, keepdims=True))
            sums = jnp.sum(part, axis=1, keepdims=True)
            result = jnp.dot(part.astype(jnp.bfloat16), value, preferred_element_type=jnp.float32)
            mixed[t, :, lanes] = (result / sums).astype(jnp.bfloat16)
        for d in range(1, nt):
            gather(g, d).start()
        return carry

    lax.fori_loop(0, groups, one_group, 0)

    def gathered(g, carry):
        for d in range(1, nt):
            other = lax.rem(t + d, nt)
            at = (other, slice(None), pl.ds(pl.multiple_of(g * span, span), span))
            remote(mixed.at[at], mixed.at[at], mixed_send.at[d - 1, g], mixed_recv.at[other, g], t, s).wait_recv()
        return carry

    chip_depth = 2 * depth
    piece = chip_depth * 128 // math.gcd(chip_depth, 128)
    tile = 256 if cols % 256 == 0 else 128

    def multiply(start, first):
        feature = pl.ds(pl.multiple_of(start, piece), piece)

        def column(j, carry):
            lanes = pl.ds(pl.multiple_of(j * tile, tile), tile)
            left = mixed[:, :, feature].reshape(nt * tokens, piece)
            product = jnp.dot(left, weights[feature, lanes], preferred_element_type=jnp.float32)
            if first:
                total[:, lanes] = product
            else:
                total[:, lanes] += product
            return carry

        lax.fori_loop(0, cols // tile, column, 0)

    chip = s // 2
    half = lax.rem(s, 2)

    def partner_arrived(c):
        arrived(2 * c + 1 - half)

    if piece == chip_depth:
        for k in range(2, chips - 1):
            relay(k)
        lax.fori_loop(0, groups, gathered, 0)
        own_weight.wait()
        partner_arrived(chip)
        multiply(chip * piece, True)

        def add(k):
            for other in (chip - k, chip + k):
                @pl.when((other >= 0) & (other < chips))
                def _():
                    partner_arrived(other)
                    multiply(other * piece, False)

        for k in range(1, chips - 1):
            add(k)
        if chips > 2:
            relay(chips - 1)
        if chips > 1:
            add(chips - 1)
    else:
        for k in range(2, chips):
            relay(k)
        lax.fori_loop(0, groups, gathered, 0)
        own_weight.wait()

        def all_arrived(c, carry):
            partner_arrived(c)
            return carry

        lax.fori_loop(0, chips, all_arrived, 0)
        multiply(0, True)

        def add_piece(p, carry):
            multiply(p * piece, False)
            return carry

        lax.fori_loop(1, inner // piece, add_piece, 0)

    def back(d):
        other = lax.rem(t + d, nt)
        return remote(outgoing.at[d - 1], incoming.at[d - 1], back_send.at[d - 1], back_recv.at[d - 1], other, s)

    def own_rows(owner):
        return pl.ds(pl.multiple_of(owner * tokens, tokens), tokens)

    for d in range(1, nt):
        outgoing[d - 1] = total[own_rows(lax.rem(t + d, nt)), :].astype(jnp.bfloat16)
        back(d).start()

    def finish(owner, branch):
        lanes = pl.ds(pl.multiple_of(owner * cols, cols), cols)
        out_ref[:, lanes] = (
            hidden_ref[:, lanes].astype(jnp.float32) + gate_ref[:, lanes] * branch
        ).astype(jnp.bfloat16)

    finish(t, total[own_rows(t), :])
    for d in range(1, nt):
        back(d).wait_recv()
        finish(lax.rem(t + nt - d, nt), incoming[d - 1].astype(jnp.float32))

    for copy, sends, _ in straight + corners:
        pl.when(sends)(copy.wait_send)
    for k in range(chips):
        low, high = s - 2 * k, s + 2 * k
        pl.when((low >= 0) & (s + 2 < ns))(near(k, low, 0, k == 0).wait_send)
        pl.when((high < ns) & (s >= 2))(near(k, high, 1, k == 0).wait_send)
        pl.when(low >= 0)(pair(k, low, 0, k == 0).wait_send)
        if k > 0:
            pl.when(high < ns)(pair(k, high, 1, False).wait_send)

    def sent(g, carry):
        for d in range(1, nt):
            gather(g, d).wait_send()
        return carry

    lax.fori_loop(0, groups, sent, 0)
    for d in range(1, nt):
        back(d).wait_send()


def shards(
    hidden_in,
    queries,
    keys,
    values,
    query_gain,
    key_gain,
    reach_time,
    reach_rows,
    reach_cols,
    out_weight,
    gate,
):
    frames, rows, columns, inner = queries.shape
    width = hidden_in.shape[3]
    heads = reach_time.shape[0]
    tokens = frames * rows * columns
    nt, ns = lax.axis_size("tm"), lax.axis_size("space")
    depth, cols = out_weight.shape
    query_norm = normalize(queries, query_gain).reshape(tokens, inner)
    stacked = jnp.stack([normalize(keys, key_gain), values])
    masks = mask_table(
        frames, rows, columns,
        lax.axis_index("tm") * frames, lax.axis_index("space") * rows,
        frames * nt, rows * ns,
    )
    kind = reach_time * 6 + reach_rows * 3 + reach_cols
    group = 5 if heads % 5 == 0 else 1
    vmem = pl.BlockSpec(memory_space=pltpu.VMEM)
    hbm = pl.BlockSpec(memory_space=pl.ANY)
    dma = pltpu.SemaphoreType.DMA
    output = pl.pallas_call(
        functools.partial(kernel, heads, group),
        out_shape=jax.ShapeDtypeStruct((tokens, width), jnp.bfloat16),
        in_specs=[pl.BlockSpec(memory_space=pltpu.SMEM), vmem, vmem, vmem, vmem, hbm, hbm],
        out_specs=vmem,
        scratch_shapes=[
            pltpu.VMEM((2, frames + 2, rows + 2, columns, inner), jnp.bfloat16),
            pltpu.VMEM((depth * ns, cols), jnp.bfloat16),
            pltpu.VMEM((nt, tokens, inner), jnp.bfloat16),
            pltpu.VMEM((nt * tokens, cols), jnp.float32),
            pltpu.VMEM((nt - 1, tokens, cols), jnp.bfloat16),
            pltpu.VMEM((nt - 1, tokens, cols), jnp.bfloat16),
            dma((2,)),
            dma((8,)),
            dma((8,)),
            dma((2, ns // 2)),
            dma((2, ns // 2)),
            dma((ns,)),
            dma((nt - 1, heads // group)),
            dma((nt, heads // group)),
            dma((nt - 1,)),
            dma((nt - 1,)),
        ],
        compiler_params=pltpu.CompilerParams(
            has_side_effects=True, vmem_limit_bytes=60 * 1024 * 1024
        ),
    )(
        kind,
        query_norm,
        masks,
        hidden_in.reshape(tokens, width),
        gate.reshape(1, width),
        stacked,
        out_weight,
    )
    return output.reshape(frames, rows, columns, width)


def solution(mesh):
    in_specs = (
        P("tm", "space", None, None),
        P("tm", "space", None, None),
        P("tm", "space", None, None),
        P("tm", "space", None, None),
        P(),
        P(),
        P(),
        P(),
        P(),
        P("space", "tm"),
        P(),
    )
    out_specs = P("tm", "space", None, None)
    return jax.shard_map(shards, mesh=mesh, in_specs=in_specs, out_specs=out_specs, check_vma=False)
```

time: 404 us -> 192 us (0.48)
  waiting for transfers between devices: 266 us -> 0 us
  Pallas kernels: 0 us -> 174 us
  blocking collectives: 34.9 us -> 0 us
  local copies, waits for them, and re-layouts: 28.3 us -> 3.29 us
  matrix products: 23.3 us -> 0 us
  other arithmetic: 26.2 us -> 11.6 us
  between operations: 13.7 us -> 0.12 us
  starting transfers between devices: 11.3 us -> 0 us
    all_gather x2 -> x0, waiting for transfers between devices: 209 us -> none  [the longest x1 123 us: shards(): gathered_rows = lax.all_gather(out_weight, 'space', axis=0, tiled=True)]
    pallas_call x0 -> x1, Pallas kernels: none -> 174 us  [shards(): pl.pallas_call(functools.partial(kernel, heads, group), out_shape=jax.Sha...]
    ppermute x4 -> x0, waiting for transfers between devices: 56.4 us -> none  [passed_along(): return lax.ppermute(block, axis, route)]
    all_to_all x1 -> x0, blocking collectives: 34.9 us -> none  [shards(): lax.all_to_all(group_terms, 'tm', split_axis=0, concat_axis=1, tiled=True)]
    dot_general x3 -> x0, matrix products: 23.3 us -> none  [the longest x1 11.5 us: shards(): jnp.dot(lax.all_gather(attention, 'tm', axis=0, tiled=True), gathered_row...]
    slice x2 -> x0, local copies, waits for them, and re-layouts: 11.8 us -> none  [the longest x1 9.06 us: shards(): region[1]]
    concatenate x2 -> x0, other arithmetic: 11.8 us -> none  [the longest x1 8.94 us: shards(): region = jnp.concatenate([below_rows, framed, above_rows], axis=2)]
    ppermute x4 -> x0, starting transfers between devices: 11.3 us -> none  [passed_along(): return lax.ppermute(block, axis, route)]
  transfers between devices with their start and end apart: 6 -> 0, of which waited for: 5 -> 0; matrix products, arithmetic and copies ran while one was open for 1% -> 0% of each run, Pallas kernels for 0% -> 0%
where the time goes in v2:
time: 192 us; the launch traced here: 189 us
  Pallas kernels  174 us (91%)
  other arithmetic  11.6 us (6%)
  local copies, waits for them, and re-layouts  3.29 us (2%)
    pallas_call x1, Pallas kernels, shards(): pl.pallas_call(functools.partial(kernel, heads, group), out_shape=jax.Sha...  174 us

profile of v2, /device:TPU:0, one launch (start us, length us, event | category | flops | bytes accessed | tf_op | source)
XLA Modules:
  0.0 189.2 jit_solution(15082557263629335859)
XLA Ops:
  0.0 1.4 add_add_fusion.kind_ref
  1.4 0.1 broadcast_in_dim.21
  1.5 0.1 sub.77
  1.6 0.1 broadcast_in_dim.20
  1.7 0.1 sub.73
  1.7 0.1 sub.82
  1.8 1.7 fusion
  3.5 1.8 fusion.3
  5.3 0.1 sub.84
  5.4 0.1 broadcast_in_dim.19
  5.5 0.1 reshape.199
  5.5 0.1 broadcast_in_dim.18
  5.6 0.1 reshape.198
  5.7 0.1 subtract_abs_fusion.2
  5.8 0.1 subtract_abs_fusion
  6.0 0.0 copy-start.2
  6.0 0.4 fusion.6
  6.4 0.0 copy-done.1
  6.4 0.0 copy-done.4
  6.4 1.4 fusion.2
  7.9 1.8 pad_maximum_fusion.kv_ref
  9.7 2.8 %and_select_fusion.mask_ref = f32[12,128,512]{2,1,0:T(8,128)} fusion(s32[128,512]{1,0:T(8,128)S(1)} %get-tuple-element.5, s32[128,512]{1,0:T(8,128)S(1)} %get-tuple-element.6, s32[128,512]{1,0:T(8,128)S(1)} %subtract_abs_fusion.2, s32[12]{0:T(128)S(1)} %copy-done.5, s32[12]{0:T(128)S(1)} %copy-done.6, s32[12]{0:T(128)S(1)} %copy-done.7, ...), kind=kLoop, calls=%fused_computation.4 | loop fusion | flops 5505024 | bytes 3932816 | tf_op jit(solution)/shard_map/jit(_where)/select_n | solution.py:52
  12.5 174.2 %shard_map.118 = bf16[128,5120]{1,0:T(8,128)(2,1)} custom-call(s32[40]{0:T(128)} %add_add_fusion.kind_ref, bf16[128,5120]{1,0:T(8,128)(2,1)} %bitcast.7, f32[12,128,512]{2,1,0:T(8,128)} %and_select_fusion.mask_ref, bf16[128,5120]{1,0:T(8,128)(2,1)} %bitcast.10, f32[1,5120]{1,0:T(1,128)} %bitcast.11, bf16[2,2,2,32,5120]{4,3,2,1,0:T(8,128)(2,1)} %pad_maximum_fusion.kv_ref, ...), custom_call_target="tpu_custom_call" | custom-call | tf_op jit(solution)/shard_map/pallas_call | solution.py:380
  186.8 2.5 %copy.14 = bf16[2,2,32,5120]{3,2,1,0:T(8,128)(2,1)} copy(bf16[2,2,32,5120]{3,2,1,0:T(8,128)(2,1)} %bitcast.8) | data formatting | bytes 2621440
  (23 shorter events, 0.1 us)
Async XLA Ops:
  0.0 6.0 %copy-start = (bf16[2,2,32,5120]{3,2,1,0:T(8,128)(2,1)S(1)}, bf16[2,2,32,5120]{3,2,1,0:T(8,128)(2,1)}, u32[]{:S(2)}) copy-start(bf16[2,2,32,5120]{3,2,1,0:T(8,128)(2,1)} %param.14) | copy-start | bytes 3932164
  0.0 6.0 %copy-start.3 = (f32[5120]{0:T(1024)S(1)}, f32[5120]{0:T(1024)}, u32[]{:S(2)}) copy-start(f32[5120]{0:T(1024)} %param.17) | copy-start | bytes 61444
  3.5 2.9 %copy-start.1 = (bf16[2,2,32,5120]{3,2,1,0:T(8,128)(2,1)S(1)}, bf16[2,2,32,5120]{3,2,1,0:T(8,128)(2,1)}, u32[]{:S(2)}) copy-start(bf16[2,2,32,5120]{3,2,1,0:T(8,128)(2,1)} %param.13) | copy-start | bytes 3932164
  3.5 2.9 %copy-start.4 = (f32[5120]{0:T(1024)S(1)}, f32[5120]{0:T(1024)}, u32[]{:S(2)}) copy-start(f32[5120]{0:T(1024)} %param.16) | copy-start | bytes 61444
  6.0 1.9 copy-start.2
  7.9 1.8 copy-start.5
  7.9 1.8 copy-start.6
  7.9 1.8 copy-start.7

commit v3 on v2

v3 whole, which is shorter than its diff:
```python
import functools
import math

import jax
import jax.numpy as jnp
import numpy as np
from jax import lax
from jax.experimental import pallas as pl
from jax.experimental.pallas import tpu as pltpu
from jax.sharding import PartitionSpec as P

TW = 8
REACHES = [(a, b, c) for a in range(2) for b in range(2) for c in range(3)]


def normalized(source, gain):
    values_f = source.astype(jnp.float32)
    mean_square = jnp.mean(values_f * values_f, axis=-1, keepdims=True)
    return (values_f * lax.rsqrt(mean_square + 1e-06) * gain).astype(jnp.bfloat16)


def places(frames, rows, columns, margin):
    grid = np.meshgrid(
        np.arange(-margin, frames + margin),
        np.arange(-margin, rows + margin),
        np.arange(columns) // TW,
        indexing="ij",
    )
    return np.stack([axis.reshape(-1) for axis in grid]).astype(np.int32)


def kernel(
    heads,
    group,
    time_ref,
    rows_ref,
    cols_ref,
    raw_query_ref,
    key_ref,
    query_gain_ref,
    key_gain_ref,
    query_place_ref,
    key_place_ref,
    gate_ref,
    value_ref,
    weight_ref,
    hidden_in_ref,
    out_ref,
    query_ref,
    mask_ref,
    hidden_ref,
    region,
    weights,
    mixed,
    total,
    outgoing,
    incoming,
    local_sem,
    own_sem,
    halo_send,
    halo_recv,
    near_send,
    pair_send,
    weight_recv,
    mixed_send,
    mixed_recv,
    back_send,
    back_recv,
):
    t = lax.axis_index("tm")
    s = lax.axis_index("space")
    nt = lax.axis_size("tm")
    ns = lax.axis_size("space")
    chips = ns // 2
    frames, rows, columns, inner = value_ref.shape
    tokens = frames * rows * columns
    keys_here = (frames + 2) * (rows + 2) * columns
    width = inner // heads
    depth, cols = weight_ref.shape

    def remote(source, target, send, recv, tm, space):
        return pltpu.make_async_remote_copy(
            src_ref=source,
            dst_ref=target,
            send_sem=send,
            recv_sem=recv,
            device_id=(tm, space),
            device_id_type=pl.DeviceIdType.MESH,
        )

    has_low_t, has_high_t = t > 0, t < nt - 1
    has_low_s, has_high_s = s > 0, s < ns - 1
    own_f, own_r = pl.ds(1, frames), pl.ds(1, rows)

    def halo(i, source, target, tm, space):
        return remote(source, target, halo_send.at[i], halo_recv.at[i], tm, space)

    straight = []
    for part, whole in ((1, value_ref), (0, region.at[0, own_f, own_r])):
        straight += [
            (halo(4 * part, whole.at[frames - 1], region.at[part, 0, own_r], t + 1, s), has_high_t, has_low_t),
            (halo(4 * part + 1, whole.at[0], region.at[part, frames + 1, own_r], t - 1, s), has_low_t, has_high_t),
            (halo(4 * part + 2, whole.at[:, rows - 1], region.at[part, own_f, 0], t, s + 1), has_high_s, has_low_s),
            (halo(4 * part + 3, whole.at[:, 0], region.at[part, own_f, rows + 1], t, s - 1), has_low_s, has_high_s),
        ]
    corners = []
    for i, (frame, has_frame) in enumerate(((0, has_low_t), (frames + 1, has_high_t))):
        corners.append((
            halo(8 + 2 * i, region.at[:, frame, rows], region.at[:, frame, 0], t, s + 1),
            has_frame & has_high_s, has_frame & has_low_s,
        ))
        corners.append((
            halo(9 + 2 * i, region.at[:, frame, 1], region.at[:, frame, rows + 1], t, s - 1),
            has_frame & has_low_s, has_frame & has_high_s,
        ))
    parts, lane = weights.shape[0], weights.shape[2]

    def block(b, p):
        return weights.at[p, pl.ds(pl.multiple_of(b * depth, depth), depth)]

    def own_block(p):
        return weight_ref.at[:, pl.ds(pl.multiple_of(p * lane, lane), lane)]

    partner = s + 1 - 2 * lax.rem(s, 2)

    def near(k, b, way, p, first):
        space = s + 2 if way == 0 else s - 2
        source = own_block(p) if first else block(b, p)
        return remote(source, block(b, p), near_send.at[way, k, p], weight_recv.at[b, p], t, space)

    def pair(k, b, way, p, first):
        source = own_block(p) if first else block(b, p)
        return remote(source, block(b, p), pair_send.at[way, k, p], weight_recv.at[b, p], t, partner)

    def arrived(b, p):
        remote(block(b, p), block(b, p), pair_send.at[0, 0, p], weight_recv.at[b, p], t, partner).wait_recv()

    def each_part(low, high, run):
        def body(p, carry):
            run(p)
            return carry

        lax.fori_loop(low, high, body, 0)

    for copy, sends, _ in straight[:4]:
        pl.when(sends)(copy.start)

    def first_part(p):
        pl.when(s + 2 < ns)(near(0, s, 0, p, True).start)
        pl.when(s >= 2)(near(0, s, 1, p, True).start)
        pair(0, s, 0, p, True).start()
        pltpu.make_async_copy(own_block(p), block(s, p), own_sem.at[p]).start()

    each_part(0, parts, first_part)
    own_value = pltpu.make_async_copy(value_ref, region.at[1, own_f, own_r], local_sem.at[0])
    own_value.start()
    own_hidden = pltpu.make_async_copy(hidden_in_ref, hidden_ref, local_sem.at[1])
    own_hidden.start()

    step = 16 if columns % 16 == 0 else columns
    for frame in range(frames):
        for row in range(rows):
            for column in range(0, columns, step):
                at = slice(column, column + step)
                region[0, 1 + frame, 1 + row, at] = normalized(key_ref[frame, row, at], key_gain_ref[...])

    def query_rows(i, carry):
        at = pl.ds(pl.multiple_of(i * 16, 16), 16)
        query_ref[at] = normalized(raw_query_ref[at], query_gain_ref[...])
        return carry

    lax.fori_loop(0, tokens // 16, query_rows, 0)
    for copy, sends, _ in straight[4:]:
        pl.when(sends)(copy.start)

    def clear_frame(frame):
        def run():
            for part in range(2):
                for row in range(rows + 2):
                    region[part, frame, row] = jnp.zeros((columns, inner), jnp.bfloat16)
        return run

    def clear_row(row):
        def run():
            for part in range(2):
                for frame in range(frames + 2):
                    region[part, frame, row] = jnp.zeros((columns, inner), jnp.bfloat16)
        return run

    pl.when(jnp.logical_not(has_low_t))(clear_frame(0))
    pl.when(jnp.logical_not(has_high_t))(clear_frame(frames + 1))
    pl.when(jnp.logical_not(has_low_s))(clear_row(0))
    pl.when(jnp.logical_not(has_high_s))(clear_row(rows + 1))

    frame_k, row_k, tile_k = key_place_ref[0:1], key_place_ref[1:2], key_place_ref[2:3]
    inside = (frame_k >= -t * frames) & (frame_k < (nt - t) * frames)
    inside = inside & (row_k >= -s * rows) & (row_k < (ns - s) * rows)
    outside = jnp.where(inside, 0, 9)
    frame_gap = jnp.abs(query_place_ref[:, 0:1] - frame_k) + outside
    row_gap = jnp.abs(query_place_ref[:, 1:2] - row_k)
    tile_gap = jnp.abs(query_place_ref[:, 2:3] - tile_k)
    for i, (reach_t, reach_r, reach_c) in enumerate(REACHES):
        allowed = (frame_gap <= reach_t) & (row_gap <= reach_r) & (tile_gap <= reach_c)
        mask_ref[i] = jnp.where(allowed, 0.0, -1e30)

    def relay(k, p):
        low, high = s - 2 * k, s + 2 * k

        @pl.when(low >= 0)
        def _():
            arrived(low, p)
            pl.when(s + 2 < ns)(near(k, low, 0, p, False).start)
            pair(k, low, 0, p, False).start()

        @pl.when(high < ns)
        def _():
            arrived(high, p)
            pl.when(s >= 2)(near(k, high, 1, p, False).start)
            pair(k, high, 1, p, False).start()

    def relay_parts(k, low, high):
        if 1 <= k < chips:
            each_part(low, high, functools.partial(relay, k))

    early = parts // 2
    last = chips - 1
    if last > 1:
        relay_parts(1, 0, early)
    for copy, _, receives in straight[0:2] + straight[4:6]:
        pl.when(receives)(copy.wait_recv)
    for copy, sends, _ in corners:
        pl.when(sends)(copy.start)
    for copy, _, receives in straight[2:4] + straight[6:8]:
        pl.when(receives)(copy.wait_recv)
    for copy, _, receives in corners:
        pl.when(receives)(copy.wait_recv)
    if last > 1:
        relay_parts(1, early, parts)
    own_value.wait()

    groups = heads // group
    span = group * width

    def gather(g, d):
        at = (t, slice(None), pl.ds(pl.multiple_of(g * span, span), span))
        return remote(
            mixed.at[at], mixed.at[at], mixed_send.at[d - 1, g], mixed_recv.at[t, g],
            lax.rem(t + d, nt), s,
        )

    def one_group(g, carry):
        for i in range(group):
            h = g * group + i
            lanes = pl.ds(pl.multiple_of(h * width, width), width)
            query = query_ref[:, lanes]
            key = region[0, :, :, :, lanes].reshape(keys_here, width)
            value = region[1, :, :, :, lanes].reshape(keys_here, width)
            scores = lax.dot_general(
                query, key, (((1,), (1,)), ((), ())), preferred_element_type=jnp.float32
            ) * width ** (-0.5)
            scores = scores + mask_ref[time_ref[h] * 6 + rows_ref[h] * 3 + cols_ref[h]]
            part = jnp.exp(scores - jnp.max(scores, axis=1, keepdims=True))
            sums = jnp.sum(part, axis=1, keepdims=True)
            result = jnp.dot(part.astype(jnp.bfloat16), value, preferred_element_type=jnp.float32)
            mixed[t, :, lanes] = (result / sums).astype(jnp.bfloat16)
        for d in range(1, nt):
            gather(g, d).start()
        return carry

    ahead = groups * 5 // 8
    lax.fori_loop(0, ahead, one_group, 0)
    if last > 2:
        relay_parts(2, 0, parts)
    lax.fori_loop(ahead, groups, one_group, 0)
    for k in range(3, last):
        relay_parts(k, 0, parts)

    def gathered(g, carry):
        for d in range(1, nt):
            other = lax.rem(t + d, nt)
            at = (other, slice(None), pl.ds(pl.multiple_of(g * span, span), span))
            remote(mixed.at[at], mixed.at[at], mixed_send.at[d - 1, g], mixed_recv.at[other, g], t, s).wait_recv()
        return carry

    chip_depth = 2 * depth
    piece = chip_depth * 128 // math.gcd(chip_depth, 128)

    def multiply(start, p, first):
        feature = pl.ds(pl.multiple_of(start, piece), piece)
        left = mixed[:, :, feature].reshape(nt * tokens, piece)
        product = jnp.dot(left, weights[p, feature], preferred_element_type=jnp.float32)
        if first:
            total[p] = product
        else:
            total[p] += product

    chip = s // 2
    half = lax.rem(s, 2)

    def add(k, p):
        for other in (chip - k, chip + k):
            @pl.when((other >= 0) & (other < chips))
            def _():
                arrived(2 * other + 1 - half, p)
                multiply(other * piece, p, False)

    def own_rows(owner):
        return pl.ds(pl.multiple_of(owner * tokens, tokens), tokens)

    def back(d, p):
        other = lax.rem(t + d, nt)
        return remote(
            outgoing.at[d - 1, p], incoming.at[d - 1, p], back_send.at[d - 1, p], back_recv.at[d - 1, p], other, s
        )

    def send_back(p):
        for d in range(1, nt):
            outgoing[d - 1, p] = total[p, own_rows(lax.rem(t + d, nt)), :].astype(jnp.bfloat16)
            back(d, p).start()

    def own_part(p):
        pltpu.make_async_copy(own_block(p), block(s, p), own_sem.at[p]).wait()
        arrived(partner, p)

    lax.fori_loop(0, groups, gathered, 0)
    if piece == chip_depth:
        def begin(p):
            own_part(p)
            multiply(chip * piece, p, True)
            for k in range(1, last):
                add(k, p)

        each_part(0, parts, begin)

        def conclude(p):
            if last > 0:
                relay(last, p)
                add(last, p)
            send_back(p)

        each_part(0, parts, conclude)
    else:
        def conclude(p):
            own_part(p)
            if last > 0:
                relay(last, p)
            for k in range(1, chips):
                for other in (chip - k, chip + k):
                    @pl.when((other >= 0) & (other < chips))
                    def _():
                        arrived(2 * other + 1 - half, p)
            multiply(0, p, True)

            def add_piece(i, carry):
                multiply(i * piece, p, False)
                return carry

            lax.fori_loop(1, inner // piece, add_piece, 0)
            send_back(p)

        each_part(0, parts, conclude)

    own_hidden.wait()

    def finish(owner, p, branch):
        lanes = pl.ds(pl.multiple_of(owner * cols + p * lane, lane), lane)
        out_ref[:, lanes] = (
            hidden_ref[:, lanes].astype(jnp.float32) + gate_ref[:, lanes] * branch
        ).astype(jnp.bfloat16)

    def finish_own(p):
        finish(t, p, total[p, own_rows(t), :])

    def finish_others(p):
        for d in range(1, nt):
            back(d, p).wait_recv()
            finish(lax.rem(t + nt - d, nt), p, incoming[d - 1, p].astype(jnp.float32))

    each_part(0, parts, finish_own)
    each_part(0, parts, finish_others)

    for copy, sends, _ in straight + corners:
        pl.when(sends)(copy.wait_send)
    for k in range(chips):
        low, high = s - 2 * k, s + 2 * k

        def weight_sent(p):
            pl.when((low >= 0) & (s + 2 < ns))(near(k, low, 0, p, k == 0).wait_send)
            pl.when((high < ns) & (s >= 2))(near(k, high, 1, p, k == 0).wait_send)
            pl.when(low >= 0)(pair(k, low, 0, p, k == 0).wait_send)
            if k > 0:
                pl.when(high < ns)(pair(k, high, 1, p, False).wait_send)

        each_part(0, parts, weight_sent)

    def sent(g, carry):
        for d in range(1, nt):
            gather(g, d).wait_send()
        return carry

    lax.fori_loop(0, groups, sent, 0)

    def back_sent(p):
        for d in range(1, nt):
            back(d, p).wait_send()

    each_part(0, parts, back_sent)


def shards(
    hidden_in,
    queries,
    keys,
    values,
    query_gain,
    key_gain,
    reach_time,
    reach_rows,
    reach_cols,
    out_weight,
    gate,
):
    frames, rows, columns, inner = queries.shape
    width = hidden_in.shape[3]
    heads = reach_time.shape[0]
    tokens = frames * rows * columns
    nt, ns = lax.axis_size("tm"), lax.axis_size("space")
    depth, cols = out_weight.shape
    group = 5 if heads % 5 == 0 else 1
    vmem = pl.BlockSpec(memory_space=pltpu.VMEM)
    hbm = pl.BlockSpec(memory_space=pl.ANY)
    dma = pltpu.SemaphoreType.DMA
    lane = 256 if cols % 256 == 0 else 128
    parts = cols // lane
    output = pl.pallas_call(
        functools.partial(kernel, heads, group),
        out_shape=jax.ShapeDtypeStruct((tokens, width), jnp.bfloat16),
        in_specs=[pl.BlockSpec(memory_space=pltpu.SMEM)] * 3 + [vmem] * 7 + [hbm] * 3,
        out_specs=vmem,
        scratch_shapes=[
            pltpu.VMEM((tokens, inner), jnp.bfloat16),
            pltpu.VMEM((len(REACHES), tokens, (frames + 2) * (rows + 2) * columns), jnp.float32),
            pltpu.VMEM((tokens, width), jnp.bfloat16),
            pltpu.VMEM((2, frames + 2, rows + 2, columns, inner), jnp.bfloat16),
            pltpu.VMEM((parts, depth * ns, lane), jnp.bfloat16),
            pltpu.VMEM((nt, tokens, inner), jnp.bfloat16),
            pltpu.VMEM((parts, nt * tokens, lane), jnp.float32),
            pltpu.VMEM((nt - 1, parts, tokens, lane), jnp.bfloat16),
            pltpu.VMEM((nt - 1, parts, tokens, lane), jnp.bfloat16),
            dma((2,)),
            dma((parts,)),
            dma((12,)),
            dma((12,)),
            dma((2, ns // 2, parts)),
            dma((2, ns // 2, parts)),
            dma((ns, parts)),
            dma((nt - 1, heads // group)),
            dma((nt, heads // group)),
            dma((nt - 1, parts)),
            dma((nt - 1, parts)),
        ],
        compiler_params=pltpu.CompilerParams(
            has_side_effects=True, vmem_limit_bytes=60 * 1024 * 1024
        ),
    )(
        reach_time,
        reach_rows,
        reach_cols,
        queries.reshape(tokens, inner),
        keys,
        query_gain.reshape(1, inner),
        key_gain.reshape(1, inner),
        places(frames, rows, columns, 0).T,
        places(frames, rows, columns, 1),
        gate.reshape(1, width),
        values,
        out_weight,
        hidden_in.reshape(tokens, width),
    )
    return output.reshape(frames, rows, columns, width)


def solution(mesh):
    in_specs = (
        P("tm", "space", None, None),
        P("tm", "space", None, None),
        P("tm", "space", None, None),
        P("tm", "space", None, None),
        P(),
        P(),
        P(),
        P(),
        P(),
        P("space", "tm"),
        P(),
    )
    out_specs = P("tm", "space", None, None)
    return jax.shard_map(shards, mesh=mesh, in_specs=in_specs, out_specs=out_specs, check_vma=False)
```

time: 192 us -> 171 us (0.89)
  other arithmetic: 11.6 us -> 0 us
  Pallas kernels: 174 us -> 166 us
    pallas_call x1, Pallas kernels: 174 us -> 166 us  [shards(): pl.pallas_call(functools.partial(kernel, heads, group), out_shape=jax.Sha...]
    reduce_sum x2 -> x0, other arithmetic: 3.45 us -> none  [normalize(): mean_square = jnp.mean(values_f * values_f, axis=-1, keepdims=True)]
    select_n x2 -> x0, other arithmetic: 2.84 us -> none  [the longest x1 2.83 us: mask_table(): return jnp.where(allowed, 0.0, -1e+30).astype(jnp.float32)]
    another operation x2 -> x0, other arithmetic: 2.17 us -> none  [shards(): stacked = jnp.stack([normalize(keys, key_gain), values])]
where the time goes in v3:
time: 171 us; the launch traced here: 169 us
  Pallas kernels  166 us (97%)
  local copies, waits for them, and re-layouts  2.46 us (1%)
    pallas_call x1, Pallas kernels, shards(): pl.pallas_call(functools.partial(kernel, heads, group), out_shape=jax.Sha...  166 us

profile of v3, /device:TPU:0, one launch (start us, length us, event | category | flops | bytes accessed | tf_op | source)
XLA Modules:
  0.0 168.5 jit_solution(66881350622307801)
XLA Ops:
  0.0 166.1 %shard_map.127 = bf16[128,5120]{1,0:T(8,128)(2,1)} custom-call(s32[40]{0:T(128)} %time_ref.1, s32[40]{0:T(128)} %rows_ref.1, s32[40]{0:T(128)} %cols_ref.1, bf16[128,5120]{1,0:T(8,128)(2,1)} %bitcast.7, bf16[2,2,32,5120]{3,2,1,0:T(8,128)(2,1)} %key_ref.1, f32[1,5120]{1,0:T(1,128)} %bitcast.9, f32[1,5120]{1,0:T(1,128)} %bitcast.10, ...), custom_call_target="tpu_custom_call" | custom-call | tf_op jit(solution)/shard_map/pallas_call | solution.py:435
  166.1 2.5 %copy.15 = bf16[2,2,32,5120]{3,2,1,0:T(8,128)(2,1)} copy(bf16[2,2,32,5120]{3,2,1,0:T(8,128)(2,1)} %bitcast.6) | data formatting | bytes 2621440
